TPU v7x, 32 devices: a whole 2x2x4 slice. The times are simulated.
32 devices in a mesh: group: 2 (over y), tm: 4 (over z), bl: 2 (over x), pol: 2 (over core).
Axes of the slice: x: 2, y: 2, z: 4, core: 2. Of those that a mesh axis runs over, the one named last changes fastest.
Arguments:
- visibilities: bfloat16 [1600, 256, 2, 384], P(('group', 'tm'), ('bl', 'pol')), parts along dimension 0, may hold values from -6 to 6
- flag_mask: int32 [1600], P(('group', 'tm')), parts along dimension 0, may hold values 0 or 1
- kernel_index: int32 [256], P(('bl', 'pol')), may hold values from 0 to 15
- filter_bank: float32 [2, 16, 257], replicated, may hold values from -0.875 to 0.875
Outputs:
- fringe_filtered: bfloat16 [160, 256, 2, 384], P('group', ('bl', 'pol', 'tm')), parts along dimension 0
There are 2 independent parts, one for each index of `group`. A program takes and returns all parts, laid end to end along the dimension named above; an argument that names none is the same for every part. Nothing has to cross between parts.
All inputs are finite; a program needn't handle non-finite values. No bound on the sum of `flag_mask` on one device may be relied on, other than what follows from the above.
Results may differ from a plain program's by a relative error of at most 0.001.
Values may be sent and summed in bfloat16 or wider, within the bound.
No kernel may reach another device: no remote copies, remote signals or barrier semaphores. Data moves between devices by JAX's collectives and lax.ppermute only.
A program may use at most 192 MiB of HBM per device.

v0:
```python
import jax
import jax.numpy as jnp
from jax import lax
from jax.sharding import PartitionSpec as P

TAPS = 257
AVG = 10


def padded(block, sides, width):
    for axis, dim in sides:
        count = lax.axis_size(axis)
        forward = [(i, i + 1) for i in range(count - 1)]
        backward = [(target, source) for source, target in forward]
        low = lax.ppermute(
            lax.slice_in_dim(block, block.shape[dim] - width, None, axis=dim), axis, forward
        )
        high = lax.ppermute(lax.slice_in_dim(block, 0, width, axis=dim), axis, backward)
        block = jnp.concatenate([low, block, high], axis=dim)
    return block


def select_taps(kernel_index, filter_bank):
    choices_count = filter_bank.shape[1]
    one_hot = (kernel_index[:, None] == jnp.arange(choices_count, dtype=jnp.int32)[None, :]).astype(
        jnp.float32
    )
    return jnp.einsum("bk,rkt->brt", one_hot, filter_bank, precision=lax.Precision.HIGHEST)


def make_band(kernel_taps, block_rows):
    tap_count = kernel_taps.shape[1]
    row_width = block_rows + tap_count - 1
    zero_tail = jnp.zeros((2, block_rows), jnp.float32)
    period_row = jnp.concatenate([kernel_taps, zero_tail], axis=1)
    tiled_rows = jnp.tile(period_row, (1, block_rows))[:, : block_rows * row_width]
    return tiled_rows.reshape(2, block_rows, row_width)


def filter_block(time_slab, kernel_taps, block_rows):
    band_rows = make_band(kernel_taps, block_rows)
    row_width = band_rows.shape[2]
    band_rows = band_rows.reshape(2, block_rows // AVG, AVG, row_width).sum(axis=2) * (1.0 / AVG)
    out_count = band_rows.shape[1]
    stacked = band_rows.reshape(2 * out_count, row_width)
    product = jnp.dot(
        stacked, time_slab, precision=lax.Precision.HIGHEST, preferred_element_type=jnp.float32
    )
    prod_real = product[:out_count]
    prod_imag = product[out_count:]
    channels = time_slab.shape[1] // 2
    out_real = prod_real[:, :channels] - prod_imag[:, channels:]
    out_imag = prod_real[:, channels:] + prod_imag[:, :channels]
    result = jnp.stack([out_real, out_imag], axis=1)
    return result


def per_device(visibilities, flag_mask, kernel_index, filter_bank):
    half_taps = TAPS // 2
    block_rows = visibilities.shape[0]
    masked = visibilities * flag_mask.astype(jnp.bfloat16)[:, None, None, None]
    extended = padded(masked, (("tm", 0),), half_taps)
    taps_all = select_taps(kernel_index, filter_bank)

    def per_base(base_index):
        time_slab = lax.dynamic_index_in_dim(extended, base_index, 1, False).astype(jnp.float32)
        time_slab = time_slab.reshape(extended.shape[0], -1)
        kernel_taps = lax.dynamic_index_in_dim(taps_all, base_index, 0, False)
        return filter_block(time_slab, kernel_taps, block_rows)

    filtered = lax.map(per_base, jnp.arange(visibilities.shape[1], dtype=jnp.int32))
    averaged = jnp.moveaxis(filtered, 0, 1).astype(jnp.bfloat16)
    return lax.all_to_all(averaged, "tm", split_axis=1, concat_axis=0, tiled=True)


def solution(mesh):
    placed = (
        P(("group", "tm"), ("bl", "pol"), None, None),
        P(("group", "tm")),
        P(("bl", "pol")),
        P(),
    )
    return jax.shard_map(
        per_device,
        mesh=mesh,
        in_specs=placed,
        out_specs=P("group", ("bl", "pol", "tm"), None, None),
        check_vma=False,
    )
```

profile of v0, /device:TPU:0, one launch (start us, length us, event | category | flops | bytes accessed | tf_op | source)
XLA Modules:
  0.0 985.1 jit_solution(15027337351065907888)
XLA Ops:
  0.7 25.5 %broadcast_multiply_fusion.1 = bf16[200,64,2,384]{3,2,1,0:T(2,128)(2,1)S(1)} fusion(bf16[200,64,2,384]{3,2,1,0:T(2,128)(2,1)} %param.6, bf16[200]{0:T(256)(128)(2,1)S(1)} %convert_element_type.11), kind=kLoop, calls=%fused_computation.11 | loop fusion | flops 9830400 | bytes 39322000 | tf_op jit(solution)/shard_map/mul | solution.py:61
  26.2 23.1 %fusion.6 = (bf16[128,64,2,384]{3,2,1,0:T(2,128)(2,1)}, bf16[128,64,2,384]{3,2,1,0:T(2,128)(2,1)}) fusion(bf16[200,64,2,384]{3,2,1,0:T(2,128)(2,1)S(1)} %broadcast_multiply_fusion.1), kind=kLoop, calls=%fused_computation.17 | loop fusion | bytes 50331648 | tf_op jit(solution)/shard_map/slice | solution.py:16
  49.3 9.5 collective-permute-start
  60.4 263.7 %collective-permute-done = bf16[128,64,2,384]{3,2,1,0:T(2,128)(2,1)} collective-permute-done((bf16[128,64,2,384]{3,2,1,0:T(2,128)(2,1)}, bf16[128,64,2,384]{3,2,1,0:T(2,128)(2,1)}, u32[]{:S(2)}, u32[]{:S(2)}) %collective-permute-start) | collective-permute-done | bytes 12582944 | tf_op jit(solution)/shard_map/ppermute | solution.py:15
  324.2 8.7 collective-permute-done.1
  332.8 69.3 %pad_maximum_fusion = bf16[456,64,2,384]{3,2,1,0:T(2,128)(2,1)} fusion(bf16[128,64,2,384]{3,2,1,0:T(2,128)(2,1)} %collective-permute-done.1, bf16[200,64,2,384]{3,2,1,0:T(2,128)(2,1)} %copy-done.2, bf16[128,64,2,384]{3,2,1,0:T(2,128)(2,1)} %collective-permute-done), kind=kLoop, calls=%fused_computation.10 | loop fusion | flops 44826624 | bytes 89653248 | tf_op jit(solution)/shard_map/concatenate | solution.py:19
  402.2 532.0 %while.10 = (s32[]{:T(128)}, bf16[64,20,2,384]{3,2,1,0:T(2,128)(2,1)}, s32[64]{0:T(128)S(1)}, f32[64,2,257]{2,0,1:T(8,128)S(1)}, bf16[456,64,2,384]{3,2,1,0:T(2,...) while((s32[]{:T(128)}, bf16[64,20,2,384]{3,2,1,0:T(2,128)(2,1)}, s32[64]{0:T(128)S(1)}, ...), condition=%wide.region_2.3_spmd, body=%wide.region_0.2_spmd.sunk | while | flops 168328320 | bytes 10199059 | solution.py:71
  407.7 1.6 constant_dynamic-slice_fusion.5
  416.0 1.6 constant_dynamic-slice_fusion.5
  424.3 1.6 constant_dynamic-slice_fusion.5
  432.6 1.6 constant_dynamic-slice_fusion.5
  440.9 1.6 constant_dynamic-slice_fusion.5
  449.2 1.6 constant_dynamic-slice_fusion.5
  457.5 1.6 constant_dynamic-slice_fusion.5
  465.8 1.6 constant_dynamic-slice_fusion.5
  474.1 1.6 constant_dynamic-slice_fusion.5
  482.5 1.6 constant_dynamic-slice_fusion.5
  490.8 1.6 constant_dynamic-slice_fusion.5
  499.1 1.6 constant_dynamic-slice_fusion.5
  507.4 1.6 constant_dynamic-slice_fusion.5
  515.7 1.6 constant_dynamic-slice_fusion.5
  524.0 1.6 constant_dynamic-slice_fusion.5
  532.3 1.6 constant_dynamic-slice_fusion.5
  540.6 1.6 constant_dynamic-slice_fusion.5
  549.0 1.6 constant_dynamic-slice_fusion.5
  557.3 1.6 constant_dynamic-slice_fusion.5
  565.6 1.6 constant_dynamic-slice_fusion.5
  573.9 1.6 constant_dynamic-slice_fusion.5
  582.2 1.6 constant_dynamic-slice_fusion.5
  590.5 1.6 constant_dynamic-slice_fusion.5
  598.8 1.6 constant_dynamic-slice_fusion.5
  607.1 1.6 constant_dynamic-slice_fusion.5
  615.4 1.6 constant_dynamic-slice_fusion.5
  623.8 1.6 constant_dynamic-slice_fusion.5
  632.1 1.6 constant_dynamic-slice_fusion.5
  640.4 1.6 constant_dynamic-slice_fusion.5
  740.1 1.6 constant_dynamic-slice_fusion.5
  748.4 1.6 constant_dynamic-slice_fusion.5
  756.7 1.6 constant_dynamic-slice_fusion.5
  765.1 1.6 constant_dynamic-slice_fusion.5
  773.4 1.6 constant_dynamic-slice_fusion.5
  898.0 1.6 constant_dynamic-slice_fusion.5
  906.4 1.6 constant_dynamic-slice_fusion.5
  914.7 1.6 constant_dynamic-slice_fusion.5
  923.0 1.6 constant_dynamic-slice_fusion.5
  931.3 1.6 constant_dynamic-slice_fusion.5
  934.1 48.2 %all_to_all.18 = bf16[20,64,2,384]{3,2,0,1:T(2,128)(2,1)S(1)} all-to-all(bf16[20,64,2,384]{3,2,0,1:T(2,128)(2,1)} %bitcast.45), channel_id=1, replica_groups=mesh['group'=2,'tm'=4,'bl'=2,'pol'=2] {'tm'}, dimensions={1} | all-to-all | bytes 3932160 | tf_op jit(solution)/shard_map/all_to_all | solution.py:73
  982.4 2.8 copy.11
  (1062 shorter events, 336.0 us)
Async XLA Ops:
  0.0 60.1 %copy-start = (f32[2,16,257]{2,1,0:T(8,128)S(1)}, f32[2,16,257]{2,1,0:T(8,128)}, u32[]{:S(2)}) copy-start(f32[2,16,257]{2,1,0:T(8,128)} %param.9) | copy-start | bytes 98692
  26.2 23.1 %copy-start.2 = (bf16[200,64,2,384]{3,2,1,0:T(2,128)(2,1)}, bf16[200,64,2,384]{3,2,1,0:T(2,128)(2,1)S(1)}, u32[]{:S(2)}) copy-start(bf16[200,64,2,384]{3,2,1,0:T(2,128)(2,1)S(1)} %broadcast_multiply_fusion.1) | copy-start | bytes 58982404
  26.2 33.9 %copy-start.3 = (s32[64]{0:T(128)S(1)}, s32[64]{0:T(128)}, u32[]{:S(2)}) copy-start(s32[64]{0:T(128)} %param.8) | copy-start | bytes 772
  49.3 274.9 %collective-permute-start = (bf16[128,64,2,384]{3,2,1,0:T(2,128)(2,1)}, bf16[128,64,2,384]{3,2,1,0:T(2,128)(2,1)}, u32[]{:S(2)}, u32[]{:S(2)}) collective-permute-start(bf16[128,64,2,384]{3,2,1,0:T(2,128)(2,1)} %get-tuple-element.60), channel_id=1, source_target_pairs={{0,4},{4,8},{8,12},{1,5},{5,9},{9,13},{2,6},{6,10},{10,14},{3,7},{... | collective-permute-start | bytes 37748744 | tf_op jit(solution)/shard_map/ppermute | solution.py:15
  58.8 274.0 %collective-permute-start.1 = (bf16[128,64,2,384]{3,2,1,0:T(2,128)(2,1)}, bf16[128,64,2,384]{3,2,1,0:T(2,128)(2,1)}, u32[]{:S(2)}, u32[]{:S(2)}) collective-permute-start(bf16[128,64,2,384]{3,2,1,0:T(2,128)(2,1)} %get-tuple-element.61), channel_id=1, source_target_pairs={{4,0},{8,4},{12,8},{5,1},{9,5},{13,9},{6,2},{10,6},{14,10},{7,3},{... | collective-permute-start | bytes 37748744 | tf_op jit(solution)/shard_map/ppermute | solution.py:18
  934.1 51.0 %copy-start.1 = (f32[2,16,257]{2,1,0:T(8,128)S(1)}, f32[2,16,257]{2,1,0:T(8,128)}, u32[]{:S(2)}) copy-start(f32[2,16,257]{2,1,0:T(8,128)} %param.9) | copy-start | bytes 98692
where the time goes:
time: 990 us; the launch traced here: 985 us
  local copies, waits for them, and re-layouts  373 us (38%)
  waiting for transfers between devices  272 us (27%)
  loops' own time  136 us (14%)
  other arithmetic  115 us (12%)
  blocking collectives  48.2 us (5%)
  matrix products  29 us (3%)
  starting transfers between devices  10.8 us (1%)
    ppermute x1, waiting for transfers between devices, padded(): lax.ppermute(lax.slice_in_dim(block, block.shape[dim] - width, None, axis...  264 us
    another operation x1, loops' own time, per_device(): lax.map(per_base, jnp.arange(visibilities.shape[1], dtype=jnp.int32))  136 us
    dynamic_slice x64, local copies, waits for them, and re-layouts, per_base(): lax.dynamic_index_in_dim(extended, base_index, 1, False).astype(jnp.float32)  102 us
    another operation x128, local copies, waits for them, and re-layouts, make_band(): jnp.tile(period_row, (1, block_rows))[:, :block_rows * row_width]  78.5 us
    reshape x64, local copies, waits for them, and re-layouts, filter_block(): band_rows.reshape(2, block_rows // AVG, AVG, row_width).sum(axis=2)  73.2 us
    concatenate x1, other arithmetic, padded(): block = jnp.concatenate([low, block, high], axis=dim)  69.3 us
    all_to_all x1, blocking collectives, per_device(): lax.all_to_all(averaged, 'tm', split_axis=1, concat_axis=0, tiled=True)  48.2 us
    dynamic_slice x64, local copies, waits for them, and re-layouts, per_device(): lax.map(per_base, jnp.arange(visibilities.shape[1], dtype=jnp.int32))  41.2 us
  transfers between devices with their start and end apart: 2, of which 2 were waited for; matrix products, arithmetic and copies ran while one was open for 0% of the time, Pallas kernels for 0%

commit v1 on v0

--- a/solution.py
+++ b/solution.py
@@ -5,6 +5,12 @@
 
 TAPS = 257
 AVG = 10
+
+
+def stacked_exchange(x, axis, split, join):
+    shards = jnp.split(x, lax.axis_size(axis), axis=split)
+    received = lax.all_to_all(jnp.stack(shards), axis, 0, 0)
+    return jnp.concatenate(received, axis=join)
 
 
 def padded(block, sides, width):
@@ -70,7 +76,7 @@
 
     filtered = lax.map(per_base, jnp.arange(visibilities.shape[1], dtype=jnp.int32))
     averaged = jnp.moveaxis(filtered, 0, 1).astype(jnp.bfloat16)
-    return lax.all_to_all(averaged, "tm", split_axis=1, concat_axis=0, tiled=True)
+    return stacked_exchange(averaged, "tm", 1, 0)
 
 
 def solution(mesh):

time: 990 us -> 1080 us (1.091)
  local copies, waits for them, and re-layouts: 373 us -> 472 us
    dynamic_update_slice x64 -> x128, local copies, waits for them, and re-layouts: 41 us -> 140 us  [per_device(): lax.map(per_base, jnp.arange(visibilities.shape[1], dtype=jnp.int32))]
where the time goes in v1:
time: 1080 us
  local copies, waits for them, and re-layouts  472 us (44%)
  waiting for transfers between devices  272 us (25%)
  loops' own time  130 us (12%)
  other arithmetic  115 us (11%)
  blocking collectives  47 us (4%)
  matrix products  28.9 us (3%)
  starting transfers between devices  10.8 us (1%)
    ppermute x1, waiting for transfers between devices, padded(): lax.ppermute(lax.slice_in_dim(block, block.shape[dim] - width, None, axis...  264 us
    dynamic_update_slice x128, local copies, waits for them, and re-layouts, per_device(): lax.map(per_base, jnp.arange(visibilities.shape[1], dtype=jnp.int32))  140 us
    another operation x1, loops' own time, per_device(): lax.map(per_base, jnp.arange(visibilities.shape[1], dtype=jnp.int32))  130 us
    dynamic_slice x64, local copies, waits for them, and re-layouts, per_base(): lax.dynamic_index_in_dim(extended, base_index, 1, False).astype(jnp.float32)  102 us
    another operation x128, local copies, waits for them, and re-layouts, make_band(): jnp.tile(period_row, (1, block_rows))[:, :block_rows * row_width]  78.5 us
    reshape x64, local copies, waits for them, and re-layouts, filter_block(): band_rows.reshape(2, block_rows // AVG, AVG, row_width).sum(axis=2)  73.2 us
    concatenate x1, other arithmetic, padded(): block = jnp.concatenate([low, block, high], axis=dim)  69.4 us
    all_to_all x1, blocking collectives, stacked_exchange(): received = lax.all_to_all(jnp.stack(shards), axis, 0, 0)  47 us
  transfers between devices with their start and end apart: 2, of which 2 were waited for; matrix products, arithmetic and copies ran while one was open for 0% of the time, Pallas kernels for 0%

profile of v1, /device:TPU:0, one launch (start us, length us, event | category | flops | bytes accessed | tf_op | source)
XLA Modules:
  0.0 1076.3 jit_solution(120123997905132549)
XLA Ops:
  0.7 25.5 %broadcast_multiply_fusion.1 = bf16[200,64,2,384]{3,2,1,0:T(2,128)(2,1)S(1)} fusion(bf16[200,64,2,384]{3,2,1,0:T(2,128)(2,1)} %param.6, bf16[200]{0:T(256)(128)(2,1)S(1)} %convert_element_type.11), kind=kLoop, calls=%fused_computation.10 | loop fusion | flops 9830400 | bytes 39322000 | tf_op jit(solution)/shard_map/mul | solution.py:67
  26.2 23.0 %fusion.6 = (bf16[128,64,2,384]{3,2,1,0:T(2,128)(2,1)}, bf16[128,64,2,384]{3,2,1,0:T(2,128)(2,1)}) fusion(bf16[200,64,2,384]{3,2,1,0:T(2,128)(2,1)S(1)} %broadcast_multiply_fusion.1), kind=kLoop, calls=%fused_computation.21 | loop fusion | bytes 50331648 | tf_op jit(solution)/shard_map/slice | solution.py:22
  49.3 9.5 collective-permute-start
  60.4 263.7 %collective-permute-done = bf16[128,64,2,384]{3,2,1,0:T(2,128)(2,1)} collective-permute-done((bf16[128,64,2,384]{3,2,1,0:T(2,128)(2,1)}, bf16[128,64,2,384]{3,2,1,0:T(2,128)(2,1)}, u32[]{:S(2)}, u32[]{:S(2)}) %collective-permute-start) | collective-permute-done | bytes 12582944 | tf_op jit(solution)/shard_map/ppermute | solution.py:21
  324.1 8.6 collective-permute-done.1
  332.8 69.4 %pad_maximum_fusion = bf16[456,64,2,384]{3,2,1,0:T(2,128)(2,1)} fusion(bf16[128,64,2,384]{3,2,1,0:T(2,128)(2,1)} %collective-permute-done.1, bf16[200,64,2,384]{3,2,1,0:T(2,128)(2,1)} %copy-done.2, bf16[128,64,2,384]{3,2,1,0:T(2,128)(2,1)} %collective-permute-done), kind=kLoop, calls=%fused_computation.9 | loop fusion | flops 44826624 | bytes 89653248 | tf_op jit(solution)/shard_map/concatenate | solution.py:25
  402.2 622.2 %while.10 = (s32[]{:T(128)}, bf16[64,20,2,384]{3,0,2,1:T(8,128)(2,1)}, s32[64]{0:T(128)S(1)}, f32[64,2,257]{2,0,1:T(8,128)S(1)}, bf16[456,64,2,384]{3,2,1,0:T(2,...) while((s32[]{:T(128)}, bf16[64,20,2,384]{3,0,2,1:T(8,128)(2,1)}, s32[64]{0:T(128)S(1)}, ...), condition=%wide.region_2.3_spmd, body=%wide.region_0.2_spmd.sunk | while | flops 168328320 | bytes 10259991 | solution.py:77
  409.8 2.1 dynamic_update_slice.5
  419.5 2.1 dynamic_update_slice.5
  438.9 2.1 dynamic_update_slice.5
  448.7 2.1 dynamic_update_slice.5
  468.1 2.1 dynamic_update_slice.5
  477.8 2.1 dynamic_update_slice.5
  487.5 2.1 dynamic_update_slice.5
  507.0 2.1 dynamic_update_slice.5
  516.7 2.1 dynamic_update_slice.5
  526.4 2.1 dynamic_update_slice.5
  545.9 2.1 dynamic_update_slice.5
  555.6 2.1 dynamic_update_slice.5
  565.3 2.1 dynamic_update_slice.5
  584.7 2.1 dynamic_update_slice.5
  594.5 2.1 dynamic_update_slice.5
  604.2 2.1 dynamic_update_slice.5
  623.6 2.1 dynamic_update_slice.5
  633.3 2.1 dynamic_update_slice.5
  643.1 2.1 dynamic_update_slice.5
  662.5 2.1 dynamic_update_slice.5
  672.2 2.1 dynamic_update_slice.5
  681.9 2.1 dynamic_update_slice.5
  701.4 2.1 dynamic_update_slice.5
  711.1 2.1 dynamic_update_slice.5
  720.8 2.1 dynamic_update_slice.5
  740.3 2.1 dynamic_update_slice.5
  750.0 2.1 dynamic_update_slice.5
  759.7 2.1 dynamic_update_slice.5
  779.1 2.1 dynamic_update_slice.5
  788.9 2.1 dynamic_update_slice.5
  798.6 2.1 dynamic_update_slice.5
  818.0 2.1 dynamic_update_slice.5
  827.7 2.1 dynamic_update_slice.5
  837.5 2.1 dynamic_update_slice.5
  856.9 2.1 dynamic_update_slice.5
  866.6 2.1 dynamic_update_slice.5
  876.4 2.1 dynamic_update_slice.5
  954.2 2.1 dynamic_update_slice.5
  1022.3 2.1 dynamic_update_slice.5
  1026.5 47.0 %all_to_all.5 = bf16[4,20,16,2,384]{4,2,3,1,0:T(8,128)(2,1)S(1)} all-to-all(bf16[4,20,16,2,384]{4,2,3,1,0:T(8,128)(2,1)S(1)} %pad_maximum_fusion.1), channel_id=1, replica_groups=mesh['group'=2,'tm'=4,'bl'=2,'pol'=2] {'tm'}, dimensions={0} | all-to-all | bytes 3932160 | tf_op jit(solution)/shard_map/all_to_all | solution.py:12
  1073.4 2.8 copy.11
  (1128 shorter events, 413.5 us)
Async XLA Ops:
  0.0 60.1 %copy-start = (f32[2,16,257]{2,1,0:T(8,128)S(1)}, f32[2,16,257]{2,1,0:T(8,128)}, u32[]{:S(2)}) copy-start(f32[2,16,257]{2,1,0:T(8,128)} %param.9) | copy-start | bytes 98692
  26.2 23.1 %copy-start.2 = (bf16[200,64,2,384]{3,2,1,0:T(2,128)(2,1)}, bf16[200,64,2,384]{3,2,1,0:T(2,128)(2,1)S(1)}, u32[]{:S(2)}) copy-start(bf16[200,64,2,384]{3,2,1,0:T(2,128)(2,1)S(1)} %broadcast_multiply_fusion.1) | copy-start | bytes 58982404
  26.2 33.9 %copy-start.3 = (s32[64]{0:T(128)S(1)}, s32[64]{0:T(128)}, u32[]{:S(2)}) copy-start(s32[64]{0:T(128)} %param.8) | copy-start | bytes 772
  49.3 274.9 %collective-permute-start = (bf16[128,64,2,384]{3,2,1,0:T(2,128)(2,1)}, bf16[128,64,2,384]{3,2,1,0:T(2,128)(2,1)}, u32[]{:S(2)}, u32[]{:S(2)}) collective-permute-start(bf16[128,64,2,384]{3,2,1,0:T(2,128)(2,1)} %get-tuple-element.60), channel_id=1, source_target_pairs={{0,4},{4,8},{8,12},{1,5},{5,9},{9,13},{2,6},{6,10},{10,14},{3,7},{... | collective-permute-start | bytes 37748744 | tf_op jit(solution)/shard_map/ppermute | solution.py:21
  58.8 274.0 %collective-permute-start.1 = (bf16[128,64,2,384]{3,2,1,0:T(2,128)(2,1)}, bf16[128,64,2,384]{3,2,1,0:T(2,128)(2,1)}, u32[]{:S(2)}, u32[]{:S(2)}) collective-permute-start(bf16[128,64,2,384]{3,2,1,0:T(2,128)(2,1)} %get-tuple-element.61), channel_id=1, source_target_pairs={{4,0},{8,4},{12,8},{5,1},{9,5},{13,9},{6,2},{10,6},{14,10},{7,3},{... | collective-permute-start | bytes 37748744 | tf_op jit(solution)/shard_map/ppermute | solution.py:24
  1024.4 51.9 %copy-start.1 = (f32[2,16,257]{2,1,0:T(8,128)S(1)}, f32[2,16,257]{2,1,0:T(8,128)}, u32[]{:S(2)}) copy-start(f32[2,16,257]{2,1,0:T(8,128)} %param.9) | copy-start | bytes 98692
